TPU v7x, 32 devices: a whole 2x2x4 slice. The times are simulated.
32 devices in a mesh: parts: 2 (over y), ep: 16 (over z, x, core).
Axes of the slice: x: 2, y: 2, z: 4, core: 2. Of those that a mesh axis runs over, the one named last changes fastest.
Arguments:
- tokens: bfloat16 [512, 2048], P(('parts', 'ep')), parts along dimension 0, may hold values from -6 to 6
- gate_up: bfloat16 [4096, 16, 1536], P(('parts', 'ep')), parts along dimension 0, may hold values from -0.125 to 0.125
- down_proj: bfloat16 [1536, 16, 2048], P(('parts', 'ep')), parts along dimension 0, may hold values from -0.21875 to 0.21875
- expert_ids: int32 [512, 8], P(('parts', 'ep')), parts along dimension 0, may hold values from 0 to 15, all different within a row; in each aligned block of 16 rows (0 to 15, 16 to 31, ...) at most 16 rows name the same one
- gate_weights: float32 [512, 8], P(('parts', 'ep')), parts along dimension 0, may hold values from 0.03 to 0.6
- owner_slot: int32 [32], P('parts'), parts along dimension 0, may hold values from 0 to 15, each once
Outputs:
- moe_out: bfloat16 [512, 2048], P(('parts', 'ep')), parts along dimension 0
- channel_scale: float32 [32, 3584], P(('parts', 'ep')), parts along dimension 0
There are 2 independent parts, one for each index of `parts`. A program takes and returns all parts, laid end to end along the dimension named above; each array names one. Nothing has to cross between parts.
Inputs may be any that keep to these rules, and one draw needn't show every extreme that they name: `expert_ids`: each row names 8 different experts; among the rows of one device no expert is named more than 16 times, a bound that some block reaches. `owner_slot`: A permutation: each slot holds exactly one expert.
All inputs are finite; a program needn't handle non-finite values.
Results may differ from a plain program's by a relative error of at most 0.0058.
Values may be sent and summed in bfloat16 or wider, within the bound.
A program may use at most 128 MiB of HBM per device.

v0:
```python
import math
import jax
import jax.numpy as jnp
from jax import lax
from jax.sharding import PartitionSpec as P


def expert_block(arrived, held_up, held_down):
    hidden = jnp.einsum("rjd,djf->rjf", arrived, held_up, preferred_element_type=jnp.float32)
    ffn_width = held_up.shape[2] // 2
    activated = (jax.nn.silu(hidden[..., :ffn_width]) * hidden[..., ffn_width:]).astype(
        jnp.bfloat16
    )
    return jnp.einsum(
        "rjf,fjd->rjd", activated, held_down, preferred_element_type=jnp.float32
    ).astype(jnp.bfloat16)


def column_scales(gate_up, down_proj):
    gate_scale = jnp.max(jnp.abs(gate_up), axis=0).astype(jnp.float32) * math.sqrt(gate_up.shape[0])
    down_scale = jnp.max(jnp.abs(down_proj), axis=0).astype(jnp.float32) * math.sqrt(
        down_proj.shape[0]
    )
    return jnp.concatenate([gate_scale, down_scale], axis=1)


def shards(tokens, gate_up, down_proj, expert_ids, gate_weights, owner_slot):
    tok_rows, model_width = tokens.shape
    top_count = expert_ids.shape[1]
    slots_all = gate_up.shape[1]
    devices = lax.axis_size("ep")
    own_count = slots_all // devices
    capacity = 2 * tok_rows * top_count // slots_all
    experts_iota = jnp.arange(slots_all, dtype=jnp.int32)
    inverse = jnp.zeros((slots_all,), jnp.int32).at[owner_slot].set(experts_iota)
    flat_ids = expert_ids.reshape(-1)
    one_hot = (flat_ids[:, None] == experts_iota[None, :]).astype(jnp.int32)
    slot_rank = jnp.sum((jnp.cumsum(one_hot, axis=0) - 1) * one_hot, axis=1)
    position = slot_rank * slots_all + flat_ids
    source_rows = jnp.repeat(tokens, top_count, axis=0)
    outbox = (
        jnp.zeros((capacity * slots_all, model_width), jnp.bfloat16).at[position].set(source_rows)
    )
    outbox = outbox.reshape(capacity, slots_all, model_width)
    held_up, held_down = (
        lax.all_to_all(gate_up, "ep", split_axis=1, concat_axis=0, tiled=True),
        lax.all_to_all(down_proj, "ep", split_axis=1, concat_axis=0, tiled=True),
    )
    arrived = lax.all_to_all(outbox, "ep", split_axis=1, concat_axis=0, tiled=True)
    expert_out = expert_block(arrived, held_up, held_down)
    returned = lax.all_to_all(expert_out, "ep", split_axis=0, concat_axis=1, tiled=True).reshape(
        capacity * slots_all, model_width
    )
    picked = returned[position].astype(jnp.float32).reshape(tok_rows, top_count, model_width)
    moe_out = jnp.sum(picked * gate_weights[:, :, None], axis=1).astype(jnp.bfloat16)
    scales = column_scales(held_up, held_down)
    every_row = lax.all_gather(scales, "ep", axis=0, tiled=True)
    mine = lax.dynamic_slice_in_dim(inverse, lax.axis_index("ep") * own_count, own_count)
    scales = jnp.take(every_row, mine, axis=0)
    return (moe_out, scales)


def solution(mesh):
    in_specs = (
        P(("parts", "ep"), None),
        P(("parts", "ep"), None, None),
        P(("parts", "ep"), None, None),
        P(("parts", "ep"), None),
        P(("parts", "ep"), None),
        P("parts"),
    )
    out_specs = (P(("parts", "ep"), None), P(("parts", "ep"), None))
    return jax.shard_map(shards, mesh=mesh, in_specs=in_specs, out_specs=out_specs, check_vma=False)
```

profile of v0, /device:TPU:9, one launch (start us, length us, event | category | flops | bytes accessed | tf_op | source)
XLA Modules:
  0.0 312.8 jit_solution(7199482188254444874)
XLA Ops:
  0.6 0.8 copy.33
  2.1 1.7 scatter_custom_fusion
  3.8 1.6 copy.35
  5.4 6.5 %all-to-all-start = ((bf16[16,16,2048]{2,0,1:T(8,128)(2,1)}), bf16[16,16,2048]{2,0,1:T(8,128)(2,1)}, u32[]{:S(2)}, u32[]{:S(2)}) async-start(bf16[16,16,2048]{2,0,1:T(8,128)(2,1)} %copy.35), calls=%async_computation | async-start | bytes 2097152 | tf_op jit(solution)/shard_map/all_to_all | solution.py:49
  12.0 8.9 %copy.36 = bf16[128,16,1536]{2,0,1:T(8,128)(2,1)} copy(bf16[128,16,1536]{2,1,0:T(8,128)(2,1)} %param.7) | data formatting | bytes 12582912 | tf_op args[1]
  20.9 16.1 %all-to-all-done = bf16[16,16,2048]{2,0,1:T(8,128)(2,1)} async-done(((bf16[16,16,2048]{2,0,1:T(8,128)(2,1)}), bf16[16,16,2048]{2,0,1:T(8,128)(2,1)}, u32[]{:S(2)}, u32[]{:S(2)}) %all-to-all-start) | async-done | bytes 1048608 | tf_op jit(solution)/shard_map/all_to_all | solution.py:49
  37.0 4.8 %all-to-all-start.1 = ((bf16[128,16,1536]{2,0,1:T(8,128)(2,1)}), bf16[128,16,1536]{2,0,1:T(8,128)(2,1)}, u32[]{:S(2)}, u32[]{:S(2)}) async-start(bf16[128,16,1536]{2,0,1:T(8,128)(2,1)} %copy.36), calls=%async_computation.1 | async-start | bytes 12582912 | tf_op jit(solution)/shard_map/all_to_all | solution.py:46
  41.8 3.4 %copy.37 = bf16[48,16,2048]{2,0,1:T(8,128)(2,1)} copy(bf16[48,16,2048]{2,1,0:T(8,128)(2,1)S(1)} %copy-done.1) | data formatting | bytes 6291456 | tf_op args[2]
  45.2 131.7 %all-to-all-done.1 = bf16[128,16,1536]{2,0,1:T(8,128)(2,1)} async-done(((bf16[128,16,1536]{2,0,1:T(8,128)(2,1)}), bf16[128,16,1536]{2,0,1:T(8,128)(2,1)}, u32[]{:S(2)}, u32[]{:S(2)}) %all-to-all-start.1) | async-done | bytes 6291488 | tf_op jit(solution)/shard_map/all_to_all | solution.py:46
  176.9 7.0 %all-to-all-start.2 = ((bf16[48,16,2048]{2,0,1:T(8,128)(2,1)}), bf16[48,16,2048]{2,0,1:T(8,128)(2,1)S(1)}, u32[]{:S(2)}, u32[]{:S(2)}) async-start(bf16[48,16,2048]{2,0,1:T(8,128)(2,1)} %copy.37), calls=%async_computation.2 | async-start | bytes 6291456 | tf_op jit(solution)/shard_map/all_to_all | solution.py:47
  184.0 0.6 scatter_custom_fusion.1
  187.2 6.1 %convolution_bitcast_fusion = f32[256,1,1536]{2,0,1:T(8,128)} fusion(bf16[256,2048]{1,0:T(8,128)(2,1)} %bitcast.6, bf16[2048,1536]{1,0:T(8,128)(2,1)} %bitcast.9), kind=kOutput, calls=%fused_computation.7 | convolution fusion | flops 1610612736 | bytes 8912896 | tf_op jit(solution)/shard_map/rjd,djf->rjf/dot_general | solution.py:9
  193.3 58.4 %all-to-all-done.2 = bf16[48,16,2048]{2,0,1:T(8,128)(2,1)S(1)} async-done(((bf16[48,16,2048]{2,0,1:T(8,128)(2,1)}), bf16[48,16,2048]{2,0,1:T(8,128)(2,1)S(1)}, u32[]{:S(2)}, u32[]{:S(2)}) %all-to-all-start.2) | async-done | bytes 3145760 | tf_op jit(solution)/shard_map/all_to_all | solution.py:47
  251.7 3.5 %fusion.2 = bf16[256,1,2048]{2,0,1:T(8,128)(2,1)} fusion(bf16[768,2048]{1,0:T(8,128)(2,1)S(1)} %bitcast.64, f32[256,1,1536]{2,0,1:T(8,128)} %convolution_bitcast_fusion), kind=kOutput, calls=%fused_computation.9 | convolution fusion | flops 807010304 | bytes 5767168 | tf_op jit(solution)/shard_map/rjf,fjd->rjd/dot_general | solution.py:14
  255.7 3.4 %reduce.4 = bf16[256,2048]{1,0:T(8,128)(2,1)} reduce(bf16[256,1,2048]{2,0,1:T(8,128)(2,1)} %fusion.2, bf16[]{:T(256)} %broadcast.120), dimensions={1}, to_apply=%copy.38.reduce_sub_computation | reduce | bytes 2097154 | tf_op jit(solution)/shard_map/convert_element_type | solution.py:16
  259.0 2.6 reshape.188
  261.7 6.9 %all-to-all-start.3 = ((bf16[16,2,16384]{2,1,0:T(2,128)(2,1)}), bf16[16,2,16384]{2,1,0:T(2,128)(2,1)}, u32[]{:S(2)}, u32[]{:S(2)}) async-start(bf16[16,2,16384]{2,1,0:T(2,128)(2,1)} %reshape.188), calls=%async_computation.3 | async-start | bytes 2097152 | tf_op jit(solution)/shard_map/all_to_all | solution.py:51
  269.0 3.4 %fusion = bf16[1536]{0:T(1024)(128)(2,1)S(1)} fusion(bf16[128,16,1536]{2,0,1:T(8,128)(2,1)} %all-to-all-done.1), kind=kLoop, calls=%fused_computation.4 | loop fusion | flops 6289920 | bytes 6294528 | tf_op jit(solution)/shard_map/reduce_max | solution.py:20
  272.4 32.2 %all-gather = f32[16,1,3584]{2,1,0:T(1,128)S(1)} all-gather(f32[1,1,3584]{2,1,0:T(1,128)S(1)} %maximum_bitcast_fusion), channel_id=1, replica_groups=mesh['parts'=2,'ep'=16] {'ep'}, dimensions={0}, use_global_device_ids=true | all-gather | bytes 243712 | tf_op jit(solution)/shard_map/all_gather | solution.py:57
  304.6 0.6 fusion.12
  305.2 4.3 %reshape.189 = bf16[256,1,2048]{2,1,0:T(2,128)(2,1)S(1)} reshape(bf16[16,2,16384]{2,1,0:T(2,128)(2,1)} %all-to-all-done.3) | data formatting | bytes 2097152
  309.5 0.6 copy.41
  310.7 0.9 gather_fusion
  311.7 1.1 fusion.3
  (27 shorter events, 2.8 us)
Async XLA Ops:
  0.6 1.4 copy-start
  5.4 31.6 %all-to-all-start = ((bf16[16,16,2048]{2,0,1:T(8,128)(2,1)}), bf16[16,16,2048]{2,0,1:T(8,128)(2,1)}, u32[]{:S(2)}, u32[]{:S(2)}) async-start(bf16[16,16,2048]{2,0,1:T(8,128)(2,1)} %copy.35), calls=%async_computation | async-start | bytes 2097152 | tf_op jit(solution)/shard_map/all_to_all | solution.py:49
  20.9 20.9 %copy-start.1 = (bf16[48,16,2048]{2,1,0:T(8,128)(2,1)S(1)}, bf16[48,16,2048]{2,1,0:T(8,128)(2,1)}, u32[]{:S(2)}) copy-start(bf16[48,16,2048]{2,1,0:T(8,128)(2,1)} %param.8) | copy-start | bytes 9437188
  37.0 139.9 %all-to-all-start.1 = ((bf16[128,16,1536]{2,0,1:T(8,128)(2,1)}), bf16[128,16,1536]{2,0,1:T(8,128)(2,1)}, u32[]{:S(2)}, u32[]{:S(2)}) async-start(bf16[128,16,1536]{2,0,1:T(8,128)(2,1)} %copy.36), calls=%async_computation.1 | async-start | bytes 12582912 | tf_op jit(solution)/shard_map/all_to_all | solution.py:46
  45.2 138.8 %copy-start.3 = (s32[16]{0:T(128)S(1)}, s32[16]{0:T(128)}, u32[]{:S(2)}) copy-start(s32[16]{0:T(128)} %param.11) | copy-start | bytes 196
  45.2 142.0 %copy-start.2 = (f32[16,8]{0,1:T(8,128)S(1)}, f32[16,8]{0,1:T(8,128)}, u32[]{:S(2)}) copy-start(f32[16,8]{0,1:T(8,128)} %param.10) | copy-start | bytes 1540
  176.9 74.8 %all-to-all-start.2 = ((bf16[48,16,2048]{2,0,1:T(8,128)(2,1)}), bf16[48,16,2048]{2,0,1:T(8,128)(2,1)S(1)}, u32[]{:S(2)}, u32[]{:S(2)}) async-start(bf16[48,16,2048]{2,0,1:T(8,128)(2,1)} %copy.37), calls=%async_computation.2 | async-start | bytes 6291456 | tf_op jit(solution)/shard_map/all_to_all | solution.py:47
  261.7 43.5 %all-to-all-start.3 = ((bf16[16,2,16384]{2,1,0:T(2,128)(2,1)}), bf16[16,2,16384]{2,1,0:T(2,128)(2,1)}, u32[]{:S(2)}, u32[]{:S(2)}) async-start(bf16[16,2,16384]{2,1,0:T(2,128)(2,1)} %reshape.188), calls=%async_computation.3 | async-start | bytes 2097152 | tf_op jit(solution)/shard_map/all_to_all | solution.py:51
where the time goes:
time: 314 us; the launch traced here: 313 us
  waiting for transfers between devices  206 us (66%)
  blocking collectives  32.2 us (10%)
  local copies, waits for them, and re-layouts  27.5 us (9%)
  starting transfers between devices  25.3 us (8%)
  matrix products  9.51 us (3%)
  other arithmetic  9.31 us (3%)
    all_to_all x1, waiting for transfers between devices, shards(): lax.all_to_all(gate_up, 'ep', split_axis=1, concat_axis=0, tiled=True)  132 us
    all_to_all x1, waiting for transfers between devices, shards(): lax.all_to_all(down_proj, 'ep', split_axis=1, concat_axis=0, tiled=True)  58.4 us
    all_gather x1, blocking collectives, shards(): every_row = lax.all_gather(scales, 'ep', axis=0, tiled=True)  32.2 us
    unnamed x15, local copies, waits for them, and re-layouts  20.7 us
    all_to_all x1, waiting for transfers between devices, shards(): lax.all_to_all(outbox, 'ep', split_axis=1, concat_axis=0, tiled=True)  16.1 us
    all_to_all x1, starting transfers between devices, shards(): lax.all_to_all(down_proj, 'ep', split_axis=1, concat_axis=0, tiled=True)  7.03 us
    all_to_all x1, starting transfers between devices, shards(): lax.all_to_all(expert_out, 'ep', split_axis=0, concat_axis=1, tiled=True)  6.93 us
    all_to_all x1, starting transfers between devices, shards(): lax.all_to_all(outbox, 'ep', split_axis=1, concat_axis=0, tiled=True)  6.55 us
  transfers between devices with their start and end apart: 4, of which 3 were waited for; matrix products, arithmetic and copies ran while one was open for 8% of the time, Pallas kernels for 0%

commit v1 on v0

--- a/solution.py
+++ b/solution.py
@@ -43,7 +43,10 @@
     )
     outbox = outbox.reshape(capacity, slots_all, model_width)
     held_up, held_down = (
-        lax.all_to_all(gate_up, "ep", split_axis=1, concat_axis=0, tiled=True),
+        jnp.concatenate(
+            lax.all_to_all(jnp.stack(jnp.split(gate_up, lax.axis_size("ep"), axis=1)), "ep", 0, 0),
+            axis=0,
+        ),
         lax.all_to_all(down_proj, "ep", split_axis=1, concat_axis=0, tiled=True),
     )
     arrived = lax.all_to_all(outbox, "ep", split_axis=1, concat_axis=0, tiled=True)

time: 314 us -> 328 us (1.045)
  local copies, waits for them, and re-layouts: 27.5 us -> 56.4 us
  waiting for transfers between devices: 206 us -> 190 us
    split x0 -> x1, local copies, waits for them, and re-layouts: none -> 24.6 us  [shards(): jnp.split(gate_up, lax.axis_size('ep'), axis=1)]
    all_to_all x1, waiting for transfers between devices: 16.1 us -> 0.01 us  [shards(): lax.all_to_all(outbox, 'ep', split_axis=1, concat_axis=0, tiled=True)]
    unnamed x15 -> x29, local copies, waits for them, and re-layouts: 20.7 us -> 24 us
  transfers between devices with their start and end apart: 4 -> 4, of which waited for: 3 -> 2; matrix products, arithmetic and copies ran while one was open for 8% -> 16% of each run, Pallas kernels for 0% -> 0%
where the time goes in v1:
time: 328 us; the launch traced here: 327 us
  waiting for transfers between devices  190 us (58%)
  local copies, waits for them, and re-layouts  56.4 us (17%)
  blocking collectives  32.2 us (10%)
  starting transfers between devices  26.8 us (8%)
  matrix products  9.52 us (3%)
  other arithmetic  9.3 us (3%)
    all_to_all x1, waiting for transfers between devices, shards(): lax.all_to_all(jnp.stack(jnp.split(gate_up, lax.axis_size('ep'), axis=1))...  132 us
    all_to_all x1, waiting for transfers between devices, shards(): lax.all_to_all(down_proj, 'ep', split_axis=1, concat_axis=0, tiled=True)  58.2 us
    all_gather x1, blocking collectives, shards(): every_row = lax.all_gather(scales, 'ep', axis=0, tiled=True)  32.2 us
    split x1, local copies, waits for them, and re-layouts, shards(): jnp.split(gate_up, lax.axis_size('ep'), axis=1)  24.6 us
    unnamed x29, local copies, waits for them, and re-layouts  24 us
    all_to_all x1, starting transfers between devices, shards(): lax.all_to_all(down_proj, 'ep', split_axis=1, concat_axis=0, tiled=True)  7.03 us
    all_to_all x1, starting transfers between devices, shards(): lax.all_to_all(expert_out, 'ep', split_axis=0, concat_axis=1, tiled=True)  6.93 us
  transfers between devices with their start and end apart: 4, of which 2 were waited for; matrix products, arithmetic and copies ran while one was open for 16% of the time, Pallas kernels for 0%

profile of v1, /device:TPU:9, one launch (start us, length us, event | category | flops | bytes accessed | tf_op | source)
XLA Modules:
  0.0 326.9 jit_solution(1073072240884815720)
XLA Ops:
  2.1 1.7 scatter_custom_fusion
  3.8 1.6 copy.111
  5.4 6.5 %all-to-all-start.1 = ((bf16[16,16,2048]{2,0,1:T(8,128)(2,1)}), bf16[16,16,2048]{2,0,1:T(8,128)(2,1)}, u32[]{:S(2)}, u32[]{:S(2)}) async-start(bf16[16,16,2048]{2,0,1:T(8,128)(2,1)} %copy.111), calls=%async_computation.1 | async-start | bytes 2097152 | tf_op jit(solution)/shard_map/all_to_all | solution.py:52
  12.0 24.6 %fusion.32 = (bf16[128,1,1536]{2,1,0:T(2,128)(2,1)S(1)}, bf16[128,1,1536]{2,1,0:T(2,128)(2,1)S(1)}, bf16[128,1,1536]{2,1,0:T(2,128)(2,1)S(1)}, bf16[128,1,1536]{...) fusion(bf16[128,16,1536]{2,1,0:T(8,128)(2,1)} %param.7), kind=kLoop, calls=%fused_computation.66 | loop fusion | bytes 12582912 | tf_op jit(solution)/shard_map/split | solution.py:47
  36.6 0.8 fusion.22
  40.6 0.9 fusion.17
  41.5 0.8 fusion.16
  42.3 0.8 fusion.15
  45.5 0.8 fusion.11
  49.6 6.3 %all-to-all-start = ((bf16[16,128,1,1536]{3,1,2,0:T(8,128)(2,1)}), bf16[16,128,1,1536]{3,1,2,0:T(8,128)(2,1)}, u32[]{:S(2)}, u32[]{:S(2)}) async-start(bf16[16,128,1,1536]{3,1,2,0:T(8,128)(2,1)} %fusion.7), calls=%async_computation | async-start | bytes 12582912 | tf_op jit(solution)/shard_map/all_to_all | solution.py:47
  55.9 3.4 %copy.112 = bf16[48,16,2048]{2,0,1:T(8,128)(2,1)} copy(bf16[48,16,2048]{2,1,0:T(8,128)(2,1)S(1)} %copy-done.1) | data formatting | bytes 6291456 | tf_op args[2]
  59.3 131.7 %all-to-all-done = bf16[16,128,1,1536]{3,1,2,0:T(8,128)(2,1)} async-done(((bf16[16,128,1,1536]{3,1,2,0:T(8,128)(2,1)}), bf16[16,128,1,1536]{3,1,2,0:T(8,128)(2,1)}, u32[]{:S(2)}, u32[]{:S(2)}) %all-to-all-start) | async-done | bytes 6291488 | tf_op jit(solution)/shard_map/all_to_all | solution.py:47
  191.0 7.0 %all-to-all-start.2 = ((bf16[48,16,2048]{2,0,1:T(8,128)(2,1)}), bf16[48,16,2048]{2,0,1:T(8,128)(2,1)S(1)}, u32[]{:S(2)}, u32[]{:S(2)}) async-start(bf16[48,16,2048]{2,0,1:T(8,128)(2,1)} %copy.112), calls=%async_computation.2 | async-start | bytes 6291456 | tf_op jit(solution)/shard_map/all_to_all | solution.py:50
  201.5 6.0 %convolution_bitcast_fusion = f32[256,1,1536]{0,2,1:T(8,128)} fusion(bf16[2048,1536]{1,0:T(8,128)(2,1)} %bitcast.16, bf16[256,2048]{1,0:T(8,128)(2,1)} %bitcast.23), kind=kOutput, calls=%fused_computation.6 | convolution fusion | flops 1610612736 | bytes 8912896 | tf_op jit(solution)/shard_map/rjd,djf->rjf/dot_general | solution.py:9
  207.5 58.2 %all-to-all-done.2 = bf16[48,16,2048]{2,0,1:T(8,128)(2,1)S(1)} async-done(((bf16[48,16,2048]{2,0,1:T(8,128)(2,1)}), bf16[48,16,2048]{2,0,1:T(8,128)(2,1)S(1)}, u32[]{:S(2)}, u32[]{:S(2)}) %all-to-all-start.2) | async-done | bytes 3145760 | tf_op jit(solution)/shard_map/all_to_all | solution.py:50
  265.8 3.5 %fusion.1 = bf16[256,1,2048]{2,0,1:T(8,128)(2,1)} fusion(bf16[768,2048]{1,0:T(8,128)(2,1)S(1)} %bitcast.119, f32[256,1,1536]{0,2,1:T(8,128)} %convolution_bitcast_fusion), kind=kOutput, calls=%fused_computation.8 | convolution fusion | flops 807010304 | bytes 5767168 | tf_op jit(solution)/shard_map/rjf,fjd->rjd/dot_general | solution.py:14
  269.8 3.4 %reduce.4 = bf16[256,2048]{1,0:T(8,128)(2,1)} reduce(bf16[256,1,2048]{2,0,1:T(8,128)(2,1)} %fusion.1, bf16[]{:T(256)} %broadcast.120), dimensions={1}, to_apply=%copy.113.reduce_sub_computation | reduce | bytes 2097154 | tf_op jit(solution)/shard_map/convert_element_type | solution.py:16
  273.2 2.6 reshape.189
  275.8 6.9 %all-to-all-start.3 = ((bf16[16,2,16384]{2,1,0:T(2,128)(2,1)}), bf16[16,2,16384]{2,1,0:T(2,128)(2,1)}, u32[]{:S(2)}, u32[]{:S(2)}) async-start(bf16[16,2,16384]{2,1,0:T(2,128)(2,1)} %reshape.189), calls=%async_computation.3 | async-start | bytes 2097152 | tf_op jit(solution)/shard_map/all_to_all | solution.py:54
  283.1 3.4 %abs_reduce_fusion = bf16[1536]{0:T(1024)(128)(2,1)S(1)} fusion(bf16[16,128,1,1536]{3,1,2,0:T(8,128)(2,1)} %all-to-all-done), kind=kLoop, calls=%fused_computation.3 | loop fusion | flops 6289920 | bytes 6294528 | tf_op jit(solution)/shard_map/reduce_max | solution.py:20
  286.5 32.2 %all-gather = f32[16,1,3584]{2,1,0:T(1,128)S(1)} all-gather(f32[1,1,3584]{2,1,0:T(1,128)S(1)} %maximum_bitcast_fusion), channel_id=1, replica_groups=mesh['parts'=2,'ep'=16] {'ep'}, dimensions={0}, use_global_device_ids=true | all-gather | bytes 243712 | tf_op jit(solution)/shard_map/all_gather | solution.py:60
  319.3 4.3 %reshape.190 = bf16[256,1,2048]{2,1,0:T(2,128)(2,1)S(1)} reshape(bf16[16,2,16384]{2,1,0:T(2,128)(2,1)} %all-to-all-done.3) | data formatting | bytes 2097152
  324.9 0.9 gather_fusion
  325.8 1.1 fusion.2
  (43 shorter events, 14.4 us)
Async XLA Ops:
  0.6 1.4 copy-start
  5.4 44.1 %all-to-all-start.1 = ((bf16[16,16,2048]{2,0,1:T(8,128)(2,1)}), bf16[16,16,2048]{2,0,1:T(8,128)(2,1)}, u32[]{:S(2)}, u32[]{:S(2)}) async-start(bf16[16,16,2048]{2,0,1:T(8,128)(2,1)} %copy.111), calls=%async_computation.1 | async-start | bytes 2097152 | tf_op jit(solution)/shard_map/all_to_all | solution.py:52
  49.6 6.3 %copy-start.1 = (bf16[48,16,2048]{2,1,0:T(8,128)(2,1)S(1)}, bf16[48,16,2048]{2,1,0:T(8,128)(2,1)}, u32[]{:S(2)}) copy-start(bf16[48,16,2048]{2,1,0:T(8,128)(2,1)} %param.8) | copy-start | bytes 9437188
  49.6 141.4 %all-to-all-start = ((bf16[16,128,1,1536]{3,1,2,0:T(8,128)(2,1)}), bf16[16,128,1,1536]{3,1,2,0:T(8,128)(2,1)}, u32[]{:S(2)}, u32[]{:S(2)}) async-start(bf16[16,128,1,1536]{3,1,2,0:T(8,128)(2,1)} %fusion.7), calls=%async_computation | async-start | bytes 12582912 | tf_op jit(solution)/shard_map/all_to_all | solution.py:47
  55.9 142.2 %copy-start.2 = (f32[16,8]{0,1:T(8,128)S(1)}, f32[16,8]{0,1:T(8,128)}, u32[]{:S(2)}) copy-start(f32[16,8]{0,1:T(8,128)} %param.10) | copy-start | bytes 1540
  55.9 142.2 %copy-start.3 = (s32[16]{0:T(128)S(1)}, s32[16]{0:T(128)}, u32[]{:S(2)}) copy-start(s32[16]{0:T(128)} %param.11) | copy-start | bytes 196
  191.0 74.8 %all-to-all-start.2 = ((bf16[48,16,2048]{2,0,1:T(8,128)(2,1)}), bf16[48,16,2048]{2,0,1:T(8,128)(2,1)S(1)}, u32[]{:S(2)}, u32[]{:S(2)}) async-start(bf16[48,16,2048]{2,0,1:T(8,128)(2,1)} %copy.112), calls=%async_computation.2 | async-start | bytes 6291456 | tf_op jit(solution)/shard_map/all_to_all | solution.py:50
  275.8 43.5 %all-to-all-start.3 = ((bf16[16,2,16384]{2,1,0:T(2,128)(2,1)}), bf16[16,2,16384]{2,1,0:T(2,128)(2,1)}, u32[]{:S(2)}, u32[]{:S(2)}) async-start(bf16[16,2,16384]{2,1,0:T(2,128)(2,1)} %reshape.189), calls=%async_computation.3 | async-start | bytes 2097152 | tf_op jit(solution)/shard_map/all_to_all | solution.py:54
